TPU v7x, 32 devices: a whole 2x2x4 slice. The times are simulated.
32 devices in a mesh: row: 2 (over x), col: 16 (over z, y, core).
Axes of the slice: x: 2, y: 2, z: 4, core: 2. Of those that a mesh axis runs over, the one named last changes fastest.
Arguments:
- upper_a: float32 [8, 2, 256, 16, 256], P(None, 'row', None, 'col'), may hold values from -0.375 to 0.375
- upper_b: float32 [8, 2, 256, 16, 256], P(None, 'row', None, 'col'), may hold values from -0.375 to 0.375
- right_side: float32 [8, 2, 256, 16, 256], P(None, 'row', None, 'col'), may hold values from -6 to 6
- vectors_a: float32 [8, 2, 256, 256], P(None, 'row'), may hold values from -0.375 to 0.375
- inverse_a: float32 [8, 2, 256, 256], P(None, 'row'), may hold values from -0.375 to 0.375
- values_a: float32 [8, 2, 256], P(None, 'row'), may hold values from 0.5 to 2
- vectors_b: float32 [16, 256, 256], P('col'), may hold values from -0.375 to 0.375
- inverse_b: float32 [16, 256, 256], P('col'), may hold values from -0.375 to 0.375
- values_b: float32 [16, 256], P('col'), may hold values from 0.5 to 2
Outputs:
- solved: float32 [8, 2, 256, 16, 256], P(None, 'row', None, 'col')
All inputs are finite; a program needn't handle non-finite values.
Results may differ from a plain program's by a relative error of at most 0.0001.
Values sent between devices are 32-bit elements; how exact they have to be, the bound alone decides.
A program may use at most 64 MiB of HBM per device.

v0:
```python
import jax
import jax.numpy as jnp
from jax import lax
from jax.sharding import PartitionSpec as P

FRONTS = 4


EXACT = lax.Precision.HIGHEST


def passed_along(value, axis, by):
    length = lax.axis_size(axis)
    pairs = [(i, i + by) for i in range(length) if 0 <= i + by < length]
    return lax.ppermute(value, axis, pairs)


def shifted(value, axis, steps):
    count = lax.axis_size(axis)
    pairs = [(source, (source + steps) % count) for source in range(count)]
    return lax.ppermute(value, axis, pairs)


def spread(value, axis, root):
    mine = lax.axis_index(axis) == root
    return lax.psum(jnp.where(mine, value, jnp.zeros_like(value)), axis)


def matmul(former, latter):
    return jnp.dot(former, latter, precision=EXACT, preferred_element_type=jnp.float32)


def diagonal_solve(residual, vectors_a, inverse_a, values_a, vectors_b, inverse_b, values_b):
    rotated = matmul(matmul(inverse_a, residual), vectors_b)
    scaled = rotated / (values_a[:, None] + values_b[None, :])
    return matmul(matmul(vectors_a, scaled), inverse_b)


def body(
    upper_a, upper_b, right_side, vectors_a, inverse_a, values_a, vectors_b, inverse_b, values_b
):
    row_count = lax.axis_size("row")
    col_count = lax.axis_size("col")
    row_pos = lax.axis_index("row")
    col_pos = lax.axis_index("col")
    local_blocks = right_side.shape[0]
    block_size = right_side.shape[2]
    square = (local_blocks, block_size, block_size)
    panel_a = upper_a.reshape(square)
    panel_b = upper_b.reshape(square)
    work = right_side.reshape(square)
    left_vectors = vectors_a.reshape(square)
    left_inverse = inverse_a.reshape(square)
    left_values = values_a.reshape(local_blocks, block_size)
    right_vectors = vectors_b.reshape(block_size, block_size)
    right_inverse = inverse_b.reshape(block_size, block_size)
    right_values = values_b.reshape(block_size)
    block_ids = jnp.arange(local_blocks, dtype=jnp.int32)
    global_rows = block_ids * row_count + row_pos
    offsets = list(range(-1, FRONTS - 1))
    moved_upper = {}
    for offset in offsets:
        if offset == 0:
            moved_upper[offset] = panel_a
        else:
            moved_upper[offset] = passed_along(panel_a, "col", offset)
    zero_block = jnp.zeros((1, block_size, block_size), jnp.float32)
    moved_lower = {}
    for offset in offsets:
        if offset % row_count == 0:
            arrived = panel_b
        else:
            arrived = shifted(panel_b, "row", -offset)
        block_carry = jnp.floor_divide(row_pos + offset, row_count)
        padded = jnp.concatenate([zero_block, arrived, zero_block], axis=0)
        moved_lower[offset] = lax.dynamic_slice_in_dim(padded, 1 + block_carry, local_blocks, 0)
    for offset in offsets:
        target = col_pos - offset
        slot_index = jnp.floor_divide(target - row_pos, row_count)
        present = (
            (jnp.remainder(target - row_pos, row_count) == 0) & (target >= 0) & (target < col_count)
        )
        picked = jnp.clip(slot_index, 0, local_blocks - 1)
        residual = lax.dynamic_index_in_dim(work, picked, 0, keepdims=False)
        solved = diagonal_solve(
            residual,
            lax.dynamic_index_in_dim(left_vectors, picked, 0, keepdims=False),
            lax.dynamic_index_in_dim(left_inverse, picked, 0, keepdims=False),
            lax.dynamic_index_in_dim(left_values, picked, 0, keepdims=False),
            right_vectors,
            right_inverse,
            right_values,
        )
        on_front = (block_ids == slot_index) & present
        work = jnp.where(on_front[:, None, None], solved[None], work)
        column_block = spread(solved, "row", jnp.remainder(target, row_count))
        upper_term = jnp.einsum("qab,bc->qac", moved_upper[offset], column_block, precision=EXACT)
        slot_blocks = jnp.where(on_front[:, None, None], solved[None], jnp.zeros_like(work))
        row_solved = lax.psum(slot_blocks, "col")
        lower_term = jnp.einsum("qab,qbc->qac", row_solved, moved_lower[offset], precision=EXACT)
        pending = col_pos - global_rows > offset
        work = jnp.where(pending[:, None, None], work - (upper_term + lower_term), work)
    return work.reshape(right_side.shape)


def solution(mesh):
    return jax.shard_map(
        body,
        mesh=mesh,
        in_specs=(
            P(None, "row", None, "col", None),
            P(None, "row", None, "col", None),
            P(None, "row", None, "col", None),
            P(None, "row", None, None),
            P(None, "row", None, None),
            P(None, "row", None),
            P("col", None, None),
            P("col", None, None),
            P("col", None),
        ),
        out_specs=P(None, "row", None, "col", None),
        check_vma=False,
    )
```

profile of v0, /device:TPU:28, one launch (start us, length us, event | category | flops | bytes accessed | tf_op | source)
XLA Modules:
  0.0 590.7 jit_solution(1330975827765755095)
XLA Ops:
  6.5 3.2 copy.54
  9.7 1.5 collective-permute-start.1
  11.2 1.5 copy.55
  12.8 2.0 collective-permute-start
  14.9 1.1 constant_dynamic-slice_fusion.4
  16.1 0.4 fusion.13
  16.6 0.4 convolution_divide_fusion.3
  16.9 1.3 fusion.41
  18.3 1.1 broadcast_select_fusion.7
  19.4 0.0 all-reduce.9.cloned.1.call-update
  19.4 0.0 all-reduce.11.cloned.1.call-start
  19.4 0.1 copy.10
  19.6 1.7 broadcast_select_fusion.3
  21.3 0.3 all-reduce.15.cloned.1.call-start
  21.7 6.1 %copy.11 = f32[8,1,256,1,256]{2,4,0,3,1:T(8,128)} copy(f32[8,1,256,1,256]{4,3,2,1,0:T(1,128)} %param.11) | data formatting | bytes 4194304 | tf_op args[2]
  27.8 35.3 %collective-permute-done.1 = f32[8,256,256]{2,1,0:T(8,128)} collective-permute-done((f32[8,256,256]{2,1,0:T(8,128)}, f32[8,256,256]{2,1,0:T(8,128)}, u32[]{:S(2)}, u32[]{:S(2)}) %collective-permute-start.1) | collective-permute-done | bytes 2097184 | tf_op jit(solution)/shard_map/ppermute | solution.py:21
  63.1 5.3 pad_maximum_fusion
  68.4 6.5 %fusion.26 = f32[256,8,256]{2,0,1:T(8,128)} fusion(f32[8,256,256]{2,1,0:T(8,128)} %collective-permute-done, f32[256,256]{1,0:T(8,128)} %all-reduce.9.cloned.1.call-done), kind=kOutput, calls=%fused_computation.45 | convolution fusion | flops 1610612736 | bytes 4456448 | tf_op jit(solution)/shard_map/qab,bc->qac/dot_general | solution.py:97
  74.9 74.9 %all-reduce.11.cloned.1.call-done = f32[8,256,256]{1,2,0:T(8,128)} async-done(((f32[8,256,256]{1,2,0:T(8,128)}), f32[8,256,256]{1,2,0:T(8,128)}) %all-reduce.11.cloned.1.call-update) | async-done | bytes 2097168 | tf_op jit(solution)/shard_map/psum | solution.py:99
  149.8 7.2 %subtract_select_fusion.3 = f32[8,256,256]{1,2,0:T(8,128)S(1)} fusion(f32[256,8,256]{2,0,1:T(8,128)} %fusion.26, f32[8,1,256,1,256]{2,4,0,3,1:T(8,128)} %copy.11, f32[8,256,256]{1,2,0:T(8,128)} %all-reduce.11.cloned.1.call-done, f32[10,256,256]{2,1,0:T(8,128)} %get-tuple-element.8, s32[]{:T(128)S(6)} %select_n.168, f32[256,256]{0,1:T(8,128)S(1)} %copy.10, ...), kind=kOutput, calls=%fused_computation.7 | convolution fusion | flops 1612709888 | bytes 10747924 | tf_op jit(solution)/shard_map/qab,qbc->qac/dot_general | solution.py:100
  157.0 1.3 copy-done.2
  158.3 0.4 fusion.24
  158.7 0.4 convolution_divide_fusion.2
  159.1 1.3 fusion.44
  160.5 1.1 broadcast_select_fusion.6
  161.6 0.1 copy.15
  161.7 1.7 broadcast_select_fusion.2
  163.4 0.0 all-reduce.13.cloned.1.call-start
  163.5 1.9 collective-permute-start.2
  165.5 0.0 all-reduce.13.cloned.1.call-update
  165.5 0.6 all-reduce.17.cloned.1.call-start
  166.1 99.0 %all-reduce.15.cloned.1.call-done = f32[8,256,256]{1,2,0:T(8,128)} async-done(((f32[8,256,256]{1,2,0:T(8,128)}), f32[8,256,256]{1,2,0:T(8,128)}) %all-reduce.15.cloned.1.call-update) | async-done | bytes 2097168 | tf_op jit(solution)/shard_map/psum | solution.py:99
  265.1 7.2 %fusion.5 = f32[8,256,256]{1,2,0:T(8,128)} fusion(f32[8,256,256]{1,2,0:T(8,128)} %all-reduce.15.cloned.1.call-done, f32[10,256,256]{2,1,0:T(8,128)} %get-tuple-element.7, s32[]{:T(128)S(6)} %select_n.176), kind=kOutput, calls=%fused_computation.20 | convolution fusion | flops 1610612736 | bytes 6291460 | tf_op jit(solution)/shard_map/qab,qbc->qac/dot_general | solution.py:100
  272.3 19.3 %all-reduce.13.cloned.1.call-done = f32[256,256]{1,0:T(8,128)} async-done(((f32[256,256]{1,0:T(8,128)}), f32[256,256]{1,0:T(8,128)}) %all-reduce.13.cloned.1.call-update) | async-done | bytes 262160 | tf_op jit(solution)/shard_map/psum | solution.py:26
  291.6 6.7 %subtract_select_fusion.2 = f32[8,256,256]{1,2,0:T(8,128)S(1)} fusion(f32[8,256,256]{1,2,0:T(8,128)} %fusion.5, f32[8,256,256]{1,2,0:T(8,128)} %copy-done.2, f32[256,256]{0,1:T(8,128)S(1)} %copy.15, pred[8]{0:T(512)(128)(4,1)S(1)} %compare_and_fusion.1, pred[8]{0:T(512)(128)(4,1)S(1)} %get-tuple-element.14, f32[256,256]{1,0:T(8,128)} %all-reduce.13.cloned.1.call-done, ...), kind=kOutput, calls=%fused_computation.6 | convolution fusion | flops 1612709888 | bytes 8912912 | tf_op jit(solution)/shard_map/qab,bc->qac/dot_general | solution.py:97
  298.4 1.3 copy-done.1
  299.7 0.4 fusion.21
  300.1 0.4 convolution_divide_fusion.1
  300.5 1.3 fusion.47
  301.8 1.1 broadcast_select_fusion.5
  302.9 0.1 copy.19
  303.0 0.0 all-reduce.17.cloned.1.call-update
  303.0 0.0 all-reduce.19.cloned.1.call-start
  303.1 1.6 broadcast_select_fusion.1
  304.7 0.0 all-reduce.23.cloned.1.call-start
  304.7 1.5 collective-permute-start.3
  306.3 20.2 %all-reduce.17.cloned.1.call-done = f32[256,256]{1,0:T(8,128)} async-done(((f32[256,256]{1,0:T(8,128)}), f32[256,256]{1,0:T(8,128)}) %all-reduce.17.cloned.1.call-update) | async-done | bytes 262160 | tf_op jit(solution)/shard_map/psum | solution.py:26
  326.5 6.5 %fusion.19 = f32[256,8,256]{2,0,1:T(8,128)} fusion(f32[8,256,256]{2,1,0:T(8,128)} %collective-permute-done.2, f32[256,256]{1,0:T(8,128)} %all-reduce.17.cloned.1.call-done), kind=kOutput, calls=%fused_computation.38 | convolution fusion | flops 1610612736 | bytes 4456448 | tf_op jit(solution)/shard_map/qab,bc->qac/dot_general | solution.py:97
  333.0 98.7 %all-reduce.19.cloned.1.call-done = f32[8,256,256]{1,2,0:T(8,128)} async-done(((f32[8,256,256]{1,2,0:T(8,128)}), f32[8,256,256]{1,2,0:T(8,128)}) %all-reduce.19.cloned.1.call-update) | async-done | bytes 2097168 | tf_op jit(solution)/shard_map/psum | solution.py:99
  431.7 7.2 %subtract_select_fusion.1 = f32[8,256,256]{1,2,0:T(8,128)S(1)} fusion(f32[256,8,256]{2,0,1:T(8,128)} %fusion.19, f32[8,256,256]{1,2,0:T(8,128)} %copy-done.1, f32[8,256,256]{1,2,0:T(8,128)} %all-reduce.19.cloned.1.call-done, f32[10,256,256]{2,1,0:T(8,128)} %get-tuple-element.8, s32[]{:T(128)S(6)} %select_n.184, f32[256,256]{0,1:T(8,128)S(1)} %copy.19, ...), kind=kOutput, calls=%fused_computation.5 | convolution fusion | flops 1612709888 | bytes 10747924 | tf_op jit(solution)/shard_map/qab,qbc->qac/dot_general | solution.py:100
  438.9 1.3 copy-done.3
  440.3 0.4 fusion.17
  440.7 0.4 convolution_divide_fusion
  441.1 1.3 fusion.50
  442.4 1.1 broadcast_select_fusion.4
  443.5 0.1 copy.23
  443.6 1.5 broadcast_select_fusion
  445.2 0.3 all-reduce.21.cloned.1.call-start
  445.5 0.5 all-reduce.21.cloned.1.call-update
  446.0 97.0 %all-reduce.23.cloned.1.call-done = f32[8,256,256]{1,2,0:T(8,128)} async-done(((f32[8,256,256]{1,2,0:T(8,128)}), f32[8,256,256]{1,2,0:T(8,128)}) %all-reduce.23.cloned.1.call-update) | async-done | bytes 2097168 | tf_op jit(solution)/shard_map/psum | solution.py:99
  543.0 7.0 %fusion.1 = f32[8,256,256]{1,2,0:T(8,128)} fusion(f32[8,256,256]{1,2,0:T(8,128)} %all-reduce.23.cloned.1.call-done, f32[10,256,256]{2,1,0:T(8,128)} %get-tuple-element.7, s32[]{:T(128)S(6)} %select_n.192), kind=kOutput, calls=%fused_computation.16 | convolution fusion | flops 1610612736 | bytes 6291460 | tf_op jit(solution)/shard_map/qab,qbc->qac/dot_general | solution.py:100
  550.0 19.6 %all-reduce.21.cloned.1.call-done = f32[256,256]{1,0:T(8,128)} async-done(((f32[256,256]{1,0:T(8,128)}), f32[256,256]{1,0:T(8,128)}) %all-reduce.21.cloned.1.call-update) | async-done | bytes 262160 | tf_op jit(solution)/shard_map/psum | solution.py:26
  569.7 8.0 %fusion = f32[8,1,256,1,256]{2,4,0,3,1:T(8,128)} fusion(f32[8,256,256]{1,2,0:T(8,128)} %fusion.1, f32[8,256,256]{1,2,0:T(8,128)} %copy-done.3, f32[8,256,256]{2,1,0:T(8,128)} %collective-permute-done.3, f32[256,256]{0,1:T(8,128)S(1)} %copy.23, pred[8]{0:T(512)(128)(4,1)S(1)} %compare_and_fusion.3, pred[8]{0:T(512)(128)(4,1)S(1)} %get-tuple-element.5, ...), kind=kOutput, calls=%fused_computation.8 | convolution fusion | flops 1612709888 | bytes 8912912 | tf_op jit(solution)/shard_map/qab,bc->qac/dot_general | solution.py:97
  577.6 6.0 %copy.27 = f32[8,1,256,1,256]{4,3,2,1,0:T(1,128)} copy(f32[8,1,256,1,256]{2,4,0,3,1:T(8,128)} %fusion) | data formatting | bytes 4194304 | tf_op jit(solution)/shard_map/reshape | solution.py:103
  (32 shorter events, 0.2 us)
Async XLA Ops:
  6.5 9.6 %copy-start = (f32[8,1,256,256]{3,2,1,0:T(8,128)S(1)}, f32[8,1,256,256]{3,2,1,0:T(8,128)}, u32[]{:S(2)}) copy-start(f32[8,1,256,256]{3,2,1,0:T(8,128)} %param.13) | copy-start | bytes 6291460
  6.5 61.8 %all-reduce.9.cloned.1.call-start = ((), (), s32[]{:S(2)}) async-start(), calls=%async_computation | async-start | bytes 524288 | tf_op jit(solution)/shard_map/psum | solution.py:26
  6.5 4.7 copy-start.4
  9.7 6.4 %copy-start.6 = (f32[8,1,256]{2,1,0:T(1,128)S(1)}, f32[8,1,256]{2,1,0:T(1,128)}, u32[]{:S(2)}) copy-start(f32[8,1,256]{2,1,0:T(1,128)} %param.14) | copy-start | bytes 24580
  9.7 6.8 %copy-start.7 = (f32[1,256,256]{2,1,0:T(8,128)S(1)}, f32[1,256,256]{2,1,0:T(8,128)}, u32[]{:S(2)}) copy-start(f32[1,256,256]{2,1,0:T(8,128)} %param.15) | copy-start | bytes 786436
  9.7 6.8 %copy-start.8 = (f32[1,256]{1,0:T(1,128)S(1)}, f32[1,256]{1,0:T(1,128)}, u32[]{:S(2)}) copy-start(f32[1,256]{1,0:T(1,128)} %param.17) | copy-start | bytes 3076
  9.7 53.3 %collective-permute-start.1 = (f32[8,256,256]{2,1,0:T(8,128)}, f32[8,256,256]{2,1,0:T(8,128)}, u32[]{:S(2)}, u32[]{:S(2)}) collective-permute-start(f32[8,256,256]{2,1,0:T(8,128)} %bitcast.125), channel_id=1, source_target_pairs={{0,16},{16,0},{1,17},{17,1},{2,18},{18,2},{3,19},{19,3},{4,20},{20... | collective-permute-start | bytes 6291464 | tf_op jit(solution)/shard_map/ppermute | solution.py:21
  12.8 5.5 copy-start.5
  12.8 55.6 %collective-permute-start = (f32[8,256,256]{2,1,0:T(8,128)}, f32[8,256,256]{2,1,0:T(8,128)}, u32[]{:S(2)}, u32[]{:S(2)}) collective-permute-start(f32[8,256,256]{2,1,0:T(8,128)} %bitcast.126), channel_id=1, source_target_pairs={{1,0},{2,1},{3,2},{4,3},{5,4},{6,5},{7,6},{8,7},{9,8},{10,9},{11,1... | collective-permute-start | bytes 6291464 | tf_op jit(solution)/shard_map/ppermute | solution.py:15
  19.4 130.4 %all-reduce.11.cloned.1.call-start = ((), (), s32[]{:S(2)}) async-start(), calls=%async_computation.1 | async-start | bytes 4194304 | tf_op jit(solution)/shard_map/psum | solution.py:99
  21.3 243.8 %all-reduce.15.cloned.1.call-start = ((), (), s32[]{:S(2)}) async-start(), calls=%async_computation.3 | async-start | bytes 4194304 | tf_op jit(solution)/shard_map/psum | solution.py:99
  157.0 1.4 copy-start.2
  163.4 128.2 %all-reduce.13.cloned.1.call-start = ((), (), s32[]{:S(2)}) async-start(), calls=%async_computation.2 | async-start | bytes 524288 | tf_op jit(solution)/shard_map/psum | solution.py:26
  163.5 142.8 %collective-permute-start.2 = (f32[8,256,256]{2,1,0:T(8,128)}, f32[8,256,256]{2,1,0:T(8,128)}, u32[]{:S(2)}, u32[]{:S(2)}) collective-permute-start(f32[8,256,256]{2,1,0:T(8,128)} %bitcast.126), channel_id=1, source_target_pairs={{0,1},{1,2},{2,3},{3,4},{4,5},{5,6},{6,7},{7,8},{8,9},{9,10},{10,1... | collective-permute-start | bytes 6291464 | tf_op jit(solution)/shard_map/ppermute | solution.py:15
  165.5 161.0 %all-reduce.17.cloned.1.call-start = ((), (), s32[]{:S(2)}) async-start(), calls=%async_computation.4 | async-start | bytes 524288 | tf_op jit(solution)/shard_map/psum | solution.py:26
  298.4 1.3 copy-start.1
  303.0 128.7 %all-reduce.19.cloned.1.call-start = ((), (), s32[]{:S(2)}) async-start(), calls=%async_computation.5 | async-start | bytes 4194304 | tf_op jit(solution)/shard_map/psum | solution.py:99
  304.7 238.3 %all-reduce.23.cloned.1.call-start = ((), (), s32[]{:S(2)}) async-start(), calls=%async_computation.7 | async-start | bytes 4194304 | tf_op jit(solution)/shard_map/psum | solution.py:99
  304.7 245.3 %collective-permute-start.3 = (f32[8,256,256]{2,1,0:T(8,128)}, f32[8,256,256]{2,1,0:T(8,128)}, u32[]{:S(2)}, u32[]{:S(2)}) collective-permute-start(f32[8,256,256]{2,1,0:T(8,128)} %bitcast.126), channel_id=1, source_target_pairs={{0,2},{1,3},{2,4},{3,5},{4,6},{5,7},{6,8},{7,9},{8,10},{9,11},{10,... | collective-permute-start | bytes 6291464 | tf_op jit(solution)/shard_map/ppermute | solution.py:15
  438.9 1.4 copy-start.3
  445.2 124.4 %all-reduce.21.cloned.1.call-start = ((), (), s32[]{:S(2)}) async-start(), calls=%async_computation.6 | async-start | bytes 524288 | tf_op jit(solution)/shard_map/psum | solution.py:26
Sparse Core Ops, SparseCore 0:
  19.5 30.0 all-reduce.8
  53.2 96.5 all-reduce.10
  163.5 101.5 all-reduce.14
  267.2 24.3 all-reduce.12
  303.2 23.2 all-reduce.16
  329.9 101.7 all-reduce.18
  445.3 97.6 all-reduce.22
  545.3 24.3 all-reduce.20
where the time goes:
time: 596 us; the launch traced here: 591 us
  waiting for transfers between devices  465 us (78%)
  matrix products  69.1 us (12%)
  local copies, waits for them, and re-layouts  22.5 us (4%)
  between operations  14.3 us (2%)
  other arithmetic  11.9 us (2%)
  starting transfers between devices  8.24 us (1%)
    psum x4, waiting for transfers between devices, body(): row_solved = lax.psum(slot_blocks, 'col')  370 us
    psum x4, waiting for transfers between devices, spread(): return lax.psum(jnp.where(mine, value, jnp.zeros_like(value)), axis)  59.2 us
    ppermute x1, waiting for transfers between devices, shifted(): return lax.ppermute(value, axis, pairs)  35.3 us
    dot_general x4, matrix products, body(): jnp.einsum('qab,qbc->qac', row_solved, moved_lower[offset], precision=EXACT)  28.6 us
    dot_general x4, matrix products, body(): jnp.einsum('qab,bc->qac', moved_upper[offset], column_block, precision=EX...  27.7 us
    unnamed x21, local copies, waits for them, and re-layouts  14.8 us
    dot_general x16, matrix products, matmul(): jnp.dot(former, latter, precision=EXACT, preferred_element_type=jnp.float32)  12.8 us
  transfers between devices with their start and end apart: 12, of which 8 were waited for; matrix products, arithmetic and copies ran while one was open for 12% of the time, Pallas kernels for 0%

commit v1 on v0

v1 whole, which is shorter than its diff:
```python
import functools

import jax
import jax.numpy as jnp
from jax import lax
from jax.experimental import pallas as pl
from jax.experimental.pallas import tpu as pltpu
from jax.sharding import PartitionSpec as P

FRONTS = 4
OFFSETS = tuple(range(-1, FRONTS - 1))
LAST = OFFSETS[-1]
MOVES = tuple(s for s in OFFSETS if s != 0)
EXACT = lax.Precision.HIGHEST
MESH = pl.DeviceIdType.MESH


def matmul(former, latter):
    return jnp.dot(former, latter, precision=EXACT, preferred_element_type=jnp.float32)


def split(value):
    high = value.astype(jnp.bfloat16)
    return high, (value - high.astype(jnp.float32)).astype(jnp.bfloat16)


def three(former, latter):
    fh, fl = split(former)
    lh, ll = split(latter)
    dot = functools.partial(jnp.dot, preferred_element_type=jnp.float32)
    return dot(fh, lh) + (dot(fh, ll) + dot(fl, lh))


def kernel(
    rows, cols, plane, turns, firsts,
    a_ref, b_ref, work_ref, va_ref, ia_ref, la_ref, vb_ref, ib_ref, lb_ref, out_ref,
    a_in, b_in, x_row, x_col,
    a_send, a_recv, b_send, b_recv, xc_send, xc_recv, xr_send, xr_recv,
):
    r = lax.axis_index("row")
    c = lax.axis_index("col")
    slots = a_ref.shape[0]
    total = slots * rows
    core = lax.rem(c, 2)
    place = lax.rem(c, plane)
    chips = plane // 2

    barrier = pltpu.get_barrier_semaphore()

    def greet_col(d, _):
        pl.semaphore_signal(barrier, inc=1, device_id=(r, lax.rem(c + d, cols)), device_id_type=MESH)
        return 0

    lax.fori_loop(1, cols, greet_col, 0)
    for d in range(1, rows):
        pl.semaphore_signal(barrier, inc=1, device_id=(lax.rem(r + d, rows), c), device_id_type=MESH)
    pl.semaphore_wait(barrier, cols - 1 + rows - 1)

    def remote(src, dst, send, recv, row, col):
        return pltpu.make_async_remote_copy(
            src_ref=src, dst_ref=dst, send_sem=send, recv_sem=recv,
            device_id=(row, col), device_id_type=MESH,
        )

    def a_copy(m, q):
        return remote(a_ref.at[q], a_in.at[m, q], a_send.at[m, q], a_recv.at[m, q],
                      r, lax.rem(c + MOVES[m] + cols, cols))

    def b_copy(d, q):
        to = lax.rem(r - turns[d] + rows, rows)
        return remote(b_ref.at[q], b_in.at[d, q], b_send.at[d, q], b_recv.at[d, q], to, c)

    def a_goes(m, q):
        to = c + MOVES[m]
        return (q * rows + r < c) & (to >= 0) & (to < cols)

    def b_goes(d, q):
        j = q * rows + r
        return (j < c) & (j - firsts[d] >= 0)

    def starts(step, _):
        q = slots - 1 - step
        for m in range(len(MOVES)):
            @pl.when(a_goes(m, q))
            def _():
                a_copy(m, q).start()
        for d in range(len(turns)):
            @pl.when(b_goes(d, q))
            def _():
                b_copy(d, q).start()
        return 0

    lax.fori_loop(0, slots, starts, 0)

    def front(s):
        i = c - s
        own = (i >= 0) & (i < total) & (lax.rem(i - r + rows, rows) == 0)
        q = jnp.clip((i - r + rows) // rows - 1, 0, slots - 1)
        return i, own, q

    def exists(s):
        return (c - s >= 0) & (c - s < total)

    def carrier(s):
        return lax.rem(r + s + 2 + core, 2) == 0

    def xc_copy(n, d):
        return remote(x_col.at[n], x_col.at[n], xc_send.at[n, d], xc_recv.at[n],
                      lax.rem(r + d, rows), c)

    def kind_to(kind):
        if kind == 0:
            return lax.rem(c + plane, cols)
        if kind == 1:
            return c + 1 - 2 * core
        return c - place + lax.rem(place + 2 * (kind - 1), plane)

    def kind_goes(n, q, kind):
        s = OFFSETS[n]
        i = q * rows + r
        c0 = i + s
        real = (c0 >= 0) & (c0 < cols) & carrier(s)
        mine = c0 == c
        below = c0 // plane < c // plane
        same = c0 // plane == c // plane
        to = kind_to(kind)
        holds = real & (mine | below | (same & (c0 >= 0)))
        if kind == 0:
            return holds & (c + plane < cols)
        if kind == 1:
            return holds & (to > c0)
        return real & mine & ((to > c0) | (c - place + plane < cols))

    def got(n, q):
        s = OFFSETS[n]
        c0 = q * rows + r + s
        real = (c0 >= 0) & (c0 < cols)
        same = c0 // plane == c // plane
        staged = same & carrier(s) & (c0 != c) & (c - place + plane < cols)
        return real & ((c0 < c) | staged)

    def xr_copy(n, q, kind, mine):
        src = x_col.at[n] if mine else x_row.at[n, q]
        return remote(src, x_row.at[n, q], xr_send.at[n, q, kind], xr_recv.at[n, q], r, kind_to(kind))

    kinds = [0, 1] + list(range(2, chips + 1))

    def take_a(m, q):
        a_copy(m, q).wait_recv()

    def take_x(n, q):
        xr_copy(n, q, 0, False).wait_recv()

    for n, s in enumerate(OFFSETS):
        i, own, q = front(s)

        @pl.when(own)
        def _(n=n, s=s, i=i, q=q):
            out_ref[q] = work_ref[q]
            for k in range(n):
                t = OFFSETS[k]

                @pl.when(exists(t))
                def _(k=k, t=t):
                    if t == 0:
                        part = a_ref.at[q]
                    else:
                        m = MOVES.index(t)
                        take_a(m, q)
                        part = a_in.at[m, q]
                    out_ref[q] = out_ref[q] - matmul(part[...], x_col[k])

                @pl.when(i + t >= 0)
                def _(k=k, t=t):
                    if (s - t) % 2 == 1:
                        take_x(k, q)
                    below = (i + t) // rows
                    turn = t % rows
                    if turn == 0:
                        part = b_ref.at[below]
                    else:
                        d = turns.index(turn)
                        if firsts[d] == t:
                            b_copy(d, below).wait_recv()
                        part = b_in.at[d, below]
                    out_ref[q] = out_ref[q] - matmul(x_row[k, q], part[...])

            rotated = matmul(matmul(ia_ref[q], out_ref[q]), vb_ref[...])
            scaled = rotated / (la_ref[q] + lb_ref[...])
            x_col[n] = matmul(matmul(va_ref[q], scaled), ib_ref[...])
            for d in range(1, rows):
                xc_copy(n, d).start()
            for kind in kinds:
                @pl.when(kind_goes(n, q, kind))
                def _(kind=kind):
                    xr_copy(n, q, kind, True).start()
            out_ref[q] = x_col[n]

        @pl.when(carrier(s))
        def _(n=n, s=s):
            def relay(step, _):
                q = slots - 1 - step

                @pl.when(got(n, q))
                def _():
                    take_x(n, q)
                    for kind in (0, 1):
                        @pl.when(kind_goes(n, q, kind))
                        def _(kind=kind):
                            xr_copy(n, q, kind, False).start()
                return 0

            lax.fori_loop(0, slots, relay, 0)

        @pl.when(exists(s) & jnp.logical_not(own))
        def _(n=n):
            xc_copy(n, 1).wait_recv()

    def finish(step, _):
        q = slots - 1 - step
        i = q * rows + r

        @pl.when(c - i > LAST)
        def _():
            out_ref[q] = work_ref[q]
            for n, s in enumerate(OFFSETS):
                @pl.when(exists(s))
                def _(n=n, s=s):
                    if s == 0:
                        part = a_ref.at[q]
                    else:
                        m = MOVES.index(s)
                        take_a(m, q)
                        part = a_in.at[m, q]
                    out_ref[q] = out_ref[q] - three(part[...], x_col[n])

                @pl.when(i + s >= 0)
                def _(n=n, s=s):
                    @pl.when(jnp.logical_not(carrier(s)))
                    def _():
                        take_x(n, q)
                    below = (i + s + rows) // rows - 1
                    turn = s % rows
                    if turn == 0:
                        part = b_ref.at[below]
                    else:
                        d = turns.index(turn)
                        if firsts[d] == s:
                            b_copy(d, below).wait_recv()
                        part = b_in.at[d, below]
                    out_ref[q] = out_ref[q] - three(x_row[n, q], part[...])

        @pl.when(c - i < OFFSETS[0])
        def _():
            out_ref[q] = work_ref[q]
        return 0

    lax.fori_loop(0, slots, finish, 0)

    def drain(q, _):
        for m in range(len(MOVES)):
            @pl.when(a_goes(m, q))
            def _():
                a_copy(m, q).wait_send()
        for d in range(len(turns)):
            @pl.when(b_goes(d, q))
            def _():
                b_copy(d, q).wait_send()
        for n in range(FRONTS):
            for kind in kinds:
                @pl.when(kind_goes(n, q, kind))
                def _():
                    xr_copy(n, q, kind, False).wait_send()
        return 0

    lax.fori_loop(0, slots, drain, 0)
    for n, s in enumerate(OFFSETS):
        _, own, _ = front(s)

        @pl.when(own)
        def _(n=n):
            for d in range(1, rows):
                xc_copy(n, d).wait_send()


def body(rows, cols, upper_a, upper_b, right_side, vectors_a, inverse_a, values_a, vectors_b, inverse_b, values_b):
    slots, size = right_side.shape[0], right_side.shape[2]
    square = (slots, size, size)
    turns, firsts = [], []
    for s in OFFSETS:
        if s % rows and s % rows not in turns:
            turns.append(s % rows)
            firsts.append(s)
    plane = max(2, cols // 4)
    moves, ways, kinds = len(MOVES), len(turns), plane // 2 + 1
    block = (size, size)
    out = pl.pallas_call(
        functools.partial(kernel, rows, cols, plane, tuple(turns), tuple(firsts)),
        out_shape=jax.ShapeDtypeStruct(square, jnp.float32),
        in_specs=[pl.BlockSpec(memory_space=pltpu.VMEM)] * 9,
        out_specs=pl.BlockSpec(memory_space=pltpu.VMEM),
        scratch_shapes=[
            pltpu.VMEM((moves, slots) + block, jnp.float32),
            pltpu.VMEM((ways, slots) + block, jnp.float32),
            pltpu.VMEM((FRONTS, slots) + block, jnp.float32),
            pltpu.VMEM((FRONTS,) + block, jnp.float32),
            pltpu.SemaphoreType.DMA((moves, slots)),
            pltpu.SemaphoreType.DMA((moves, slots)),
            pltpu.SemaphoreType.DMA((ways, slots)),
            pltpu.SemaphoreType.DMA((ways, slots)),
            pltpu.SemaphoreType.DMA((FRONTS, rows)),
            pltpu.SemaphoreType.DMA((FRONTS,)),
            pltpu.SemaphoreType.DMA((FRONTS, slots, kinds)),
            pltpu.SemaphoreType.DMA((FRONTS, slots)),
        ],
        compiler_params=pltpu.CompilerParams(
            collective_id=0, has_side_effects=True, vmem_limit_bytes=60 * 1024 * 1024
        ),
    )(
        upper_a.reshape(square), upper_b.reshape(square), right_side.reshape(square),
        vectors_a.reshape(square), inverse_a.reshape(square), values_a.reshape(slots, size, 1),
        vectors_b.reshape(block), inverse_b.reshape(block), values_b.reshape(1, size),
    )
    return out.reshape(right_side.shape)


def solution(mesh):
    return jax.shard_map(
        functools.partial(body, mesh.shape["row"], mesh.shape["col"]),
        mesh=mesh,
        in_specs=(
            P(None, "row", None, "col", None),
            P(None, "row", None, "col", None),
            P(None, "row", None, "col", None),
            P(None, "row", None, None),
            P(None, "row", None, None),
            P(None, "row", None),
            P("col", None, None),
            P("col", None, None),
            P("col", None),
        ),
        out_specs=P(None, "row", None, "col", None),
        check_vma=False,
    )
```

time: 596 us -> 164 us (0.28)
  waiting for transfers between devices: 465 us -> 0 us
  Pallas kernels: 0 us -> 151 us
  matrix products: 69.1 us -> 0 us
  between operations: 14.3 us -> 0.02 us
  other arithmetic: 11.9 us -> 0.72 us
  local copies, waits for them, and re-layouts: 22.5 us -> 12 us
  starting transfers between devices: 8.24 us -> 0 us
    psum x8 -> x0, waiting for transfers between devices: 429 us -> none  [the longest x4 370 us: body(): row_solved = lax.psum(slot_blocks, 'col')]
    pallas_call x0 -> x1, Pallas kernels: none -> 151 us  [body(): pl.pallas_call(functools.partial(kernel, rows, cols, plane, tuple(turns),...]
    dot_general x24 -> x0, matrix products: 69.1 us -> none  [the longest x4 28.6 us: body(): jnp.einsum('qab,qbc->qac', row_solved, moved_lower[offset], precision=EXACT)]
    ppermute x4 -> x0, waiting for transfers between devices: 35.3 us -> none  [the longest x1 35.3 us: shifted(): return lax.ppermute(value, axis, pairs)]
    unnamed x21 -> x6, local copies, waits for them, and re-layouts: 14.8 us -> 5.57 us
    ppermute x4 -> x0, starting transfers between devices: 6.92 us -> none  [the longest x3 5.43 us: passed_along(): return lax.ppermute(value, axis, pairs)]
    select_n x4 -> x0, other arithmetic: 6.51 us -> none  [body(): jnp.where(on_front[:, None, None], solved[None], jnp.zeros_like(work))]
  transfers between devices with their start and end apart: 12 -> 0, of which waited for: 8 -> 0; matrix products, arithmetic and copies ran while one was open for 12% -> 0% of each run, Pallas kernels for 0% -> 0%
where the time goes in v1:
time: 164 us
  Pallas kernels  151 us (92%)
  local copies, waits for them, and re-layouts  12 us (7%)
    pallas_call x1, Pallas kernels, body(): pl.pallas_call(functools.partial(kernel, rows, cols, plane, tuple(turns),...  151 us
    unnamed x6, local copies, waits for them, and re-layouts  5.57 us
    reshape x1, local copies, waits for them, and re-layouts, body(): return out.reshape(right_side.shape)  5.08 us

profile of v1, /device:TPU:28, one launch (start us, length us, event | category | flops | bytes accessed | tf_op | source)
XLA Modules:
  0.0 163.6 jit_solution(4777300634114582029)
XLA Ops:
  0.0 0.7 reduce
  0.7 1.3 reshape.36.la_ref
  2.1 0.0 copy-start
  2.1 0.0 copy-start.1
  2.1 3.2 %copy.19 = f32[8,1,256,1,256]{4,2,3,1,0:T(8,128)} copy(f32[8,1,256,1,256]{4,3,2,1,0:T(1,128)} %param.9) | data formatting | bytes 4194304
  5.3 0.0 copy-done
  5.3 0.0 copy-done.1
  5.3 2.4 %copy_bitcast_fusion = (f32[8,256,256]{2,1,0:T(8,128)}, f32[8,256,256]{2,1,0:T(8,128)}) fusion(f32[8,1,256,1,256]{4,3,2,1,0:T(1,128)S(1)} %copy-done, f32[8,1,256,1,256]{4,3,2,1,0:T(1,128)S(1)} %copy-done.1), kind=kLoop, calls=%fused_computation | loop fusion | bytes 8388608
  7.6 150.9 %shard_map.91 = f32[8,256,256]{2,1,0:T(8,128)} custom-call(f32[8,256,256]{2,1,0:T(8,128)} %bitcast.12, f32[8,256,256]{2,1,0:T(8,128)} %get-tuple-element.6.b_ref, f32[8,256,256]{2,1,0:T(8,128)} %get-tuple-element.5.work_ref, f32[8,256,256]{2,1,0:T(8,128)} %bitcast.14, f32[8,256,256]{2,1,0:T(8,128)} %bitcast.15, f32[8,256,1]{2,1,0:T(8,128)} %reshape.36.la_ref, ...), custom_call_target="tpu_custom_call" | custom-call | tf_op jit(solution)/shard_map/pallas_call | solution.py:297
  158.5 5.1 %copy.12 = f32[8,1,256,1,256]{4,3,2,1,0:T(1,128)} copy(f32[8,1,256,1,256]{4,2,0,3,1:T(8,128)} %bitcast.13) | data formatting | bytes 4194304 | tf_op jit(solution)/shard_map/reshape | solution.py:324
Async XLA Ops:
  2.1 3.2 %copy-start = (f32[8,1,256,1,256]{4,3,2,1,0:T(1,128)S(1)}, f32[8,1,256,1,256]{4,3,2,1,0:T(1,128)}, u32[]{:S(2)}) copy-start(f32[8,1,256,1,256]{4,3,2,1,0:T(1,128)} %param.11) | copy-start | bytes 6291460
  2.1 3.2 %copy-start.1 = (f32[8,1,256,1,256]{4,3,2,1,0:T(1,128)S(1)}, f32[8,1,256,1,256]{4,3,2,1,0:T(1,128)}, u32[]{:S(2)}) copy-start(f32[8,1,256,1,256]{4,3,2,1,0:T(1,128)} %param.10) | copy-start | bytes 6291460

commit v2 on v1

--- a/solution.py
+++ b/solution.py
@@ -78,19 +78,27 @@
         j = q * rows + r
         return (j < c) & (j - firsts[d] >= 0)
 
-    def starts(step, _):
-        q = slots - 1 - step
-        for m in range(len(MOVES)):
-            @pl.when(a_goes(m, q))
-            def _():
-                a_copy(m, q).start()
-        for d in range(len(turns)):
-            @pl.when(b_goes(d, q))
-            def _():
-                b_copy(d, q).start()
-        return 0
-
-    lax.fori_loop(0, slots, starts, 0)
+    near = LAST - OFFSETS[0]
+    bounds = (0, near + 1, near + 1 + 3 * cols // 8, total + cols)
+
+    def starts(part):
+        def one(step, _):
+            q = slots - 1 - step
+            gap = c - (q * rows + r)
+            now = (gap >= bounds[part]) & (gap < bounds[part + 1])
+            for m in range(len(MOVES)):
+                @pl.when(now & a_goes(m, q))
+                def _(m=m):
+                    a_copy(m, q).start()
+            for d in range(len(turns)):
+                @pl.when(now & b_goes(d, q))
+                def _(d=d):
+                    b_copy(d, q).start()
+            return 0
+
+        lax.fori_loop(0, slots, one, 0)
+
+    starts(0)
 
     def front(s):
         i = c - s
@@ -198,6 +206,8 @@
 
         @pl.when(carrier(s))
         def _(n=n, s=s):
+            starts(1 + n // 2)
+
             def relay(step, _):
                 q = slots - 1 - step
 

time: 164 us -> 151 us (0.921); the launches traced: 164 us -> 148 us
  Pallas kernels: 151 us -> 135 us
    pallas_call x1, Pallas kernels: 151 us -> 135 us  [body(): pl.pallas_call(functools.partial(kernel, rows, cols, plane, tuple(turns),...]
where the time goes in v2:
time: 151 us; the launch traced here: 148 us
  Pallas kernels  135 us (89%)
  local copies, waits for them, and re-layouts  12 us (8%)
    pallas_call x1, Pallas kernels, body(): pl.pallas_call(functools.partial(kernel, rows, cols, plane, tuple(turns),...  135 us
    unnamed x6, local copies, waits for them, and re-layouts  5.57 us
    reshape x1, local copies, waits for them, and re-layouts, body(): return out.reshape(right_side.shape)  5.08 us

profile of v2, /device:TPU:28, one launch (start us, length us, event | category | flops | bytes accessed | tf_op | source)
XLA Modules:
  0.0 148.1 jit_solution(11657597172900727429)
XLA Ops:
  0.0 0.7 reduce
  0.7 1.3 reshape.36.la_ref
  2.1 0.0 copy-start
  2.1 0.0 copy-start.1
  2.1 3.2 %copy.19 = f32[8,1,256,1,256]{4,2,3,1,0:T(8,128)} copy(f32[8,1,256,1,256]{4,3,2,1,0:T(1,128)} %param.9) | data formatting | bytes 4194304
  5.3 0.0 copy-done
  5.3 0.0 copy-done.1
  5.3 2.4 %copy_bitcast_fusion = (f32[8,256,256]{2,1,0:T(8,128)}, f32[8,256,256]{2,1,0:T(8,128)}) fusion(f32[8,1,256,1,256]{4,3,2,1,0:T(1,128)S(1)} %copy-done, f32[8,1,256,1,256]{4,3,2,1,0:T(1,128)S(1)} %copy-done.1), kind=kLoop, calls=%fused_computation | loop fusion | bytes 8388608
  7.6 135.4 %shard_map.91 = f32[8,256,256]{2,1,0:T(8,128)} custom-call(f32[8,256,256]{2,1,0:T(8,128)} %bitcast.12, f32[8,256,256]{2,1,0:T(8,128)} %get-tuple-element.6.b_ref, f32[8,256,256]{2,1,0:T(8,128)} %get-tuple-element.5.work_ref, f32[8,256,256]{2,1,0:T(8,128)} %bitcast.14, f32[8,256,256]{2,1,0:T(8,128)} %bitcast.15, f32[8,256,1]{2,1,0:T(8,128)} %reshape.36.la_ref, ...), custom_call_target="tpu_custom_call" | custom-call | tf_op jit(solution)/shard_map/pallas_call | solution.py:307
  143.0 5.1 %copy.12 = f32[8,1,256,1,256]{4,3,2,1,0:T(1,128)} copy(f32[8,1,256,1,256]{4,2,0,3,1:T(8,128)} %bitcast.13) | data formatting | bytes 4194304 | tf_op jit(solution)/shard_map/reshape | solution.py:334
Async XLA Ops:
  2.1 3.2 %copy-start = (f32[8,1,256,1,256]{4,3,2,1,0:T(1,128)S(1)}, f32[8,1,256,1,256]{4,3,2,1,0:T(1,128)}, u32[]{:S(2)}) copy-start(f32[8,1,256,1,256]{4,3,2,1,0:T(1,128)} %param.11) | copy-start | bytes 6291460
  2.1 3.2 %copy-start.1 = (f32[8,1,256,1,256]{4,3,2,1,0:T(1,128)S(1)}, f32[8,1,256,1,256]{4,3,2,1,0:T(1,128)}, u32[]{:S(2)}) copy-start(f32[8,1,256,1,256]{4,3,2,1,0:T(1,128)} %param.10) | copy-start | bytes 6291460
